TPU v7x, 128 devices: a whole 4x4x4 slice. The times are simulated.
128 devices in a mesh: gx: 8 (over z_hi, x), gy: 4 (over z_lo, core), gz: 4 (over y).
Axes of the slice: x: 4, y: 4, z: 4 (z_hi: 2, z_lo: 2; z = z_hi * 2 + z_lo), core: 2. Of those that a mesh axis runs over, the one named last changes fastest.
Arguments:
- calcium: float32 [8, 256, 128, 512], P(None, 'gx', 'gz', 'gy'), may hold values from 0.1 to 3
- activation: float32 [8, 256, 128, 512], P(None, 'gx', 'gz', 'gy'), may hold values from 0 to 1
- element_first: int32 [256], replicated, may hold values from 0 to 63, as said below
- offset_first: float32 [256], replicated, may hold values from 0.1 to 0.9
- element_second: int32 [512], replicated, may hold values from 0 to 127, as said below
- offset_second: float32 [512], replicated, may hold values from 0.1 to 0.9
- element_third: int32 [128], replicated, may hold values from 0 to 31, as said below
- offset_third: float32 [128], replicated, may hold values from 0.1 to 0.9
- troponin: float32 [64, 32, 128], P('gx', ('gy', 'gz')), may hold values from 0 to 1
- tension: float32 [64, 32, 128], P('gx', ('gy', 'gz')), may hold values from 0 to 2
- unbind_rate: float32 [64, 32, 128], P('gx', ('gy', 'gz')), may hold values from 0.2 to 2
- relax_rate: float32 [64, 32, 128], P('gx', ('gy', 'gz')), may hold values from 0.5 to 4
Outputs:
- bound_fraction: float32 [64, 32, 128], P('gx', ('gy', 'gz'))
- active_tension: float32 [64, 32, 128], P('gx', ('gy', 'gz'))
Inputs may be any that keep to these rules, and one draw needn't show every extreme that they name: `element_first`: never falling; the cells of each aligned block of 32 cells belong to that block's own 8 elements, each element holding at least one cell. `element_second`: never falling; the cells of each aligned block of 128 cells belong to that block's own 32 elements, each element holding at least one cell. `element_third`: never falling; the cells of each aligned block of 8 cells belong to that block's own 2 elements, each element holding at least one cell.
All inputs are finite; a program needn't handle non-finite values.
Results may differ from a plain program's by a relative error of at most 0.00005.
Values sent between devices are 32-bit elements.
No kernel may reach another device: no remote copies, remote signals or barrier semaphores. Data moves between devices by JAX's collectives and lax.ppermute only.
A program may use at most 64 MiB of HBM per device.

v0:
```python
import jax
import jax.numpy as jnp
from jax import lax
from jax.experimental import pallas as pl
from jax.experimental.pallas import tpu as pltpu
from jax.sharding import PartitionSpec as P


step_size = 0.2
bind_rate = 2.0
peak_tension = 2.0
half_square = 0.25

f32 = jnp.float32
bf16 = jnp.bfloat16
LANES = 128
SUBS = 8
NODES = 8
COLS = 32
ROWS = 72
BLOCK = 104
SURE = 28
PIECE = 72


def hat(element, offset, first_node, rows):
    cells = element.shape[0]
    element = element.reshape(1, cells)
    offset = offset.reshape(1, cells)
    node = first_node + lax.broadcasted_iota(jnp.int32, (rows, cells), 0)
    raw = jnp.where(element == node, 1.0 - offset, 0.0) + jnp.where(
        element + 1 == node, offset, 0.0
    )
    return raw / jnp.sum(raw, axis=1, keepdims=True)


def halves(value):
    high = value.astype(bf16).astype(f32)
    return high, value - high


def lane_ids(rows):
    return lax.broadcasted_iota(jnp.int32, (rows, LANES), 1)


def pick_lanes(values, index):
    return jnp.take_along_axis(values, index, axis=1, mode="promise_in_bounds")


def edge_kernel(
    calcium,
    activation,
    element_first,
    offset_first,
    element_second,
    offset_second,
    element_third,
    offset_third,
    edge,
    first_weight,
    depth_weight,
    col_high,
    col_low,
    elements_1,
    offsets_1,
    elements_2,
    offsets_2,
    elements_3,
    offsets_3,
    sure_cells,
    cells,
    sums,
    small_sems,
    sure_sem,
    cell_sems,
):
    gx, gy, gz = lax.axis_index("gx"), lax.axis_index("gy"), lax.axis_index("gz")
    small = [
        (element_first, elements_1),
        (offset_first, offsets_1),
        (element_third, elements_3),
        (offset_third, offsets_3),
        (element_second, elements_2),
        (offset_second, offsets_2),
    ]
    loads = [
        pltpu.make_async_copy(source, target, small_sems.at[n])
        for n, (source, target) in enumerate(small)
    ]
    fields = (calcium, activation)
    sure_copies = [
        pltpu.make_async_copy(field.at[:, SURE:], sure_cells.at[f], sure_sem)
        for f, field in enumerate(fields)
    ]
    for load in loads:
        load.start()
    for copy in sure_copies:
        copy.start()
    loads[0].wait()

    place = lax.broadcasted_iota(jnp.int32, (1, 256), 1)
    earlier = jnp.logical_and(
        place // 32 == gx, elements_1[...].reshape(1, 256) < gx * NODES + NODES - 1
    )
    begin = jnp.sum(jnp.where(earlier, 1.0, 0.0)).astype(jnp.int32)

    count = (SURE + 1 - begin) // 2

    def start(n, carry):
        for f, field in enumerate(fields):
            layers = pl.ds(SURE - 2 - 2 * n, 2)
            pltpu.make_async_copy(
                field.at[:, layers], cells.at[n, f], cell_sems.at[n]
            ).start()
        return carry

    lax.fori_loop(0, count, start, 0)
    loads[1].wait()
    loads[2].wait()
    loads[3].wait()

    first = hat(elements_1[...], offsets_1[...], gx * NODES, 16)
    own = jnp.where(gx >= 4, first[:, LANES:], first[:, :LANES])
    third = hat(elements_3[...], offsets_3[...], gz * NODES, 16)
    depth = pick_lanes(third, gz * 32 + lane_ids(16) % 32)
    first_weight[...] = own
    depth_weight[...] = depth

    loads[4].wait()
    loads[5].wait()
    second = hat(elements_2[...], offsets_2[...], gy * COLS, 40)
    chunk = second[:, :LANES]
    for c in range(1, 4):
        chunk = jnp.where(gy == c, second[:, c * LANES : (c + 1) * LANES], chunk)
    full = jnp.concatenate([chunk, jnp.zeros((LANES - 40, LANES), f32)], 0)
    turned = full.T
    lane = lane_ids(LANES)
    for group in range(4):
        first_lane = group * COLS
        main = turned if group == 0 else pltpu.roll(turned, first_lane, 1)
        main = jnp.where(lane // COLS == group, main, 0.0)
        shift = (first_lane - COLS) % LANES
        extra = turned if shift == 0 else pltpu.roll(turned, shift, 1)
        extra = jnp.where(lane == first_lane, extra, 0.0)
        high, low = halves(jnp.concatenate([main, extra], 1))
        rows = slice(group * LANES, (group + 1) * LANES)
        col_high[rows] = high.astype(bf16)
        col_low[rows] = low.astype(bf16)

    layer = jnp.broadcast_to(own[NODES : NODES + 1], (8, LANES))

    def cell_weight(x):
        index = jnp.full((8, LANES), lax.rem(gx, 4) * 32 + x, jnp.int32)
        return jnp.concatenate([pick_lanes(layer, index)] * 4, 0)

    slots = [(f, t, (f * SUBS + t) * LANES) for f in range(2) for t in range(SUBS)]
    pltpu.make_async_copy(sure_cells, sure_cells, sure_sem).wait()
    sure_weights = [cell_weight(x) for x in range(SURE, 32)]
    for f, t, column in slots:
        total = None
        for n, weight in enumerate(sure_weights):
            part = weight * sure_cells[f, t, n]
            total = part if total is None else total + part
        sums[:, column : column + LANES] = total

    def add(n, carry):
        pltpu.make_async_copy(cells.at[n], cells.at[n], cell_sems.at[n]).wait()
        pair = [cell_weight(SURE - 2 - 2 * n + i) for i in range(2)]
        for f, t, column in slots:
            part = pair[0] * cells[n, f, t, 0] + pair[1] * cells[n, f, t, 1]
            sums[:, column : column + LANES] += part
        return carry

    lax.fori_loop(0, count, add, 0)

    depth_high, depth_low = halves(depth[:, :32])
    weights = jnp.concatenate([depth_high, depth_low], 0).astype(bf16)
    high, low = halves(sums[...])
    upper = jnp.dot(weights, high.astype(bf16), preferred_element_type=f32)
    lower = jnp.dot(weights[:16], low.astype(bf16), preferred_element_type=f32)
    planes = upper[:16] + upper[16:] + lower
    whole = jnp.concatenate([planes[:, j * 512 : (j + 1) * 512] for j in range(4)], 0)
    result = columns(whole, col_high, col_low)
    quads = [result[j * 16 : j * 16 + 16] for j in range(4)]
    extra = quads[0][:, LANES:]
    for j in range(1, 4):
        extra = extra + pltpu.roll(quads[j][:, LANES:], j, 1)
    for j in range(4):
        edge[j * 8 : j * 8 + 8] = quads[j][:8, :LANES]
    corners = [q[8:9, :LANES] for q in quads] + [extra[8:9]]
    edge[32:40] = jnp.concatenate(corners + [jnp.zeros((3, LANES), f32)], 0)
    edge[40:48] = extra[:8]


def columns(whole, col_high, col_low):
    high, low = halves(whole)
    high, low = high.astype(bf16), low.astype(bf16)
    return (
        jnp.dot(high, col_high[...], preferred_element_type=f32)
        + jnp.dot(low, col_high[...], preferred_element_type=f32)
        + jnp.dot(high, col_low[...], preferred_element_type=f32)
    )


def restrict_kernel(
    calcium, activation, first_weight, depth_weight, col_high, col_low, blocks, pair_weight
):
    gx = lax.axis_index("gx")
    lane = lane_ids(16)
    own, depth = first_weight[...], depth_weight[...]
    for tile in range(8):
        row = pick_lanes(own, lax.rem(gx, 4) * 32 + 4 * tile + lane // 32)
        parts = [depth[b : b + 1] * row[:NODES] for b in range(NODES + 1)]
        both = jnp.concatenate(halves(jnp.concatenate(parts, 0)), 0)
        pair_weight[:, tile * LANES : (tile + 1) * LANES] = both.astype(bf16)

    cells = 32 * 32

    def section(t):
        field = jnp.concatenate(
            [calcium[t].reshape(cells, LANES), activation[t].reshape(cells, LANES)], 1
        )
        high, low = halves(field)
        upper = jnp.dot(pair_weight[...], high.astype(bf16), preferred_element_type=f32)
        lower = jnp.dot(pair_weight[:80], low.astype(bf16), preferred_element_type=f32)
        total = upper[:ROWS] + upper[ROWS:] + lower[:ROWS]
        return jnp.concatenate([total[:, :LANES], total[:, LANES:]], 0)

    packed = []
    for half in range(2):
        whole = jnp.concatenate([section(4 * half + g) for g in range(4)], 1)
        packed.append(columns(whole, col_high, col_low))
    quads = [packed[half][f * ROWS : (f + 1) * ROWS] for f in range(2) for half in range(2)]
    main = [q[:, :LANES] for q in quads]
    extra = quads[0][:, LANES:]
    for j in range(1, 4):
        extra = extra + pltpu.roll(quads[j][:, LANES:], j, 1)
    for k in range(4):
        tail = None
        for p, plane in enumerate((2 * k, 2 * k + 1, NODES)):
            rows = slice(plane * 8, plane * 8 + 8)
            for j in range(4):
                start = j * 24 + p * 8
                blocks[k, start : start + 8] = main[j][rows]
            piece = extra[rows]
            piece = piece if p == 0 else pltpu.roll(piece, 4 * p, 1)
            tail = piece if tail is None else tail + piece
        blocks[k, 96:104] = tail


def route_kernel(blocks, incoming, *outs):
    gz = lax.axis_index("gz")
    top = lax.broadcasted_iota(jnp.int32, (8, LANES), 0) == 0
    top = jnp.logical_and(top, lax.axis_index("gx") > 0)
    for k in range(4):
        which = lax.rem(gz + k, 4)
        out = outs[k]
        tail = None
        for p in range(3):
            for j in range(4):
                start = j * 24 + p * 8
                if p < 2:
                    row = incoming[pl.ds(j * 8 + 2 * which + p, 1), :]
                else:
                    row = incoming[32 + j : 33 + j, :]
                out[start : start + 8] = blocks[which, start : start + 8] + jnp.where(
                    top, row, 0.0
                )
            if p < 2:
                row = incoming[pl.ds(40 + 2 * which + p, 1), :]
            else:
                row = incoming[36:37, :]
            row = jnp.where(top, row, 0.0)
            row = row if p == 0 else pltpu.roll(row, 4 * p, 1)
            tail = row if tail is None else tail + row
        out[96:104] = blocks[which, 96:104] + tail


def combine_kernel(own, one, two, three, *rest):
    outs, slabs = rest[:4], rest[4]
    gy, gz = lax.axis_index("gy"), lax.axis_index("gz")
    for k, message in enumerate((own, one, two, three)):
        slabs[lax.rem(gz + 4 - k, 4)] = message[...]
    lane = lane_ids(8)
    for k in range(4):
        slab = lax.rem(gy + k, 4)
        before = lax.rem(slab + 3, 4)
        joins = jnp.logical_and(gz == 0, slab > 0)
        out = outs[k]
        for j in range(4):
            start = j * 24
            plane = slabs[before, start + 16 : start + 24]
            out[j * 16 : j * 16 + 8] = slabs[slab, start : start + 8] + jnp.where(
                joins, plane, 0.0
            )
            out[j * 16 + 8 : j * 16 + 16] = slabs[slab, start + 8 : start + 16]
        tail = pltpu.roll(slabs[before, 96:104], LANES - 8, 1)
        tail = jnp.where(jnp.logical_and(joins, lane % COLS < 4), tail, 0.0)
        out[64:72] = slabs[slab, 96:104] + tail


def tension_kernel(
    own, one, two, three, troponin, tension, unbind, relax, bound_out, active_out, chunks
):
    gy = lax.axis_index("gy")
    for k, message in enumerate((own, one, two, three)):
        chunks[lax.rem(gy + 4 - k, 4)] = message[...]
    lane = lane_ids(8)
    pieces = [chunks[c] for c in range(4)]

    def turn(value, shift):
        shift = shift % LANES
        return value if shift == 0 else pltpu.roll(value, shift, 1)

    def drive(f, substep, plane):
        half, group = divmod(substep, 4)
        j = 2 * f + half
        start = j * 16 + plane * 8
        total = None
        for c in range(4):
            part = turn(pieces[c][start : start + 8], COLS * (c - group))
            total = part if total is None else jnp.where(lane // COLS == c, part, total)
        for c in range(3):
            shift = COLS * (c + 1) - (COLS * group + 4 * plane + j)
            part = turn(pieces[c][64:72], shift)
            total = total + jnp.where(lane == COLS * (c + 1), part, 0.0)
        return total

    for plane in range(2):
        bound = troponin[:, plane, :]
        active = tension[:, plane, :]
        unbinding = unbind[:, plane, :]
        relaxing = step_size * relax[:, plane, :]
        for substep in range(SUBS):
            calcium_now = drive(0, substep, plane)
            squared = calcium_now * calcium_now
            binding = squared / (squared + half_square)
            bound = bound + step_size * (
                bind_rate * binding * (1.0 - bound) - unbinding * bound
            )
            active = active + relaxing * (
                peak_tension * drive(1, substep, plane) * bound - active
            )
        bound_out[:, plane, :] = bound
        active_out[:, plane, :] = active


def exchange(messages, axis):
    received = [messages[0]] + [None] * 3
    for k in range(1, 4):
        pairs = [(i, (i + k) % 4) for i in range(4)]
        received[k] = lax.ppermute(messages[k], axis, pairs)
    return received


def per_device(
    calcium,
    activation,
    element_first,
    offset_first,
    element_second,
    offset_second,
    element_third,
    offset_third,
    troponin,
    tension,
    unbind_rate,
    relax_rate,
):
    line = lambda n, kind: pltpu.VMEM((n,), kind)
    vectors = (
        element_first,
        offset_first,
        element_second,
        offset_second,
        element_third,
        offset_third,
    )
    far = [
        pltpu.with_memory_space_constraint(x, pltpu.HBM)
        for x in (calcium, activation) + vectors
    ]
    edge, *weights = pl.pallas_call(
        edge_kernel,
        in_specs=[pl.BlockSpec(memory_space=pltpu.HBM)] * 8,
        out_shape=[
            jax.ShapeDtypeStruct((48, LANES), f32),
            jax.ShapeDtypeStruct((16, LANES), f32),
            jax.ShapeDtypeStruct((16, LANES), f32),
            jax.ShapeDtypeStruct((512, 256), bf16),
            jax.ShapeDtypeStruct((512, 256), bf16),
        ],
        scratch_shapes=[line(x.shape[0], x.dtype) for x in vectors]
        + [
            pltpu.VMEM((2, SUBS, 32 - SURE, 32, LANES), f32),
            pltpu.VMEM((SURE // 2, 2, SUBS, 2, 32, LANES), f32),
            pltpu.VMEM((32, 2048), f32),
            pltpu.SemaphoreType.DMA((6,)),
            pltpu.SemaphoreType.DMA,
            pltpu.SemaphoreType.DMA((SURE // 2,)),
        ],
        compiler_params=pltpu.CompilerParams(vmem_limit_bytes=16 << 20),
        name="edge",
    )(*far)
    incoming = lax.ppermute(edge, "gx", [(i, (i + 1) % 8) for i in range(8)])
    blocks = pl.pallas_call(
        restrict_kernel,
        out_shape=jax.ShapeDtypeStruct((4, BLOCK, LANES), f32),
        scratch_shapes=[pltpu.VMEM((2 * ROWS, 1024), bf16)],
        compiler_params=pltpu.CompilerParams(vmem_limit_bytes=16 << 20),
        name="restrict",
    )(calcium, activation, *weights)
    small = pltpu.CompilerParams(vmem_limit_bytes=4 << 20)
    message = jax.ShapeDtypeStruct((BLOCK, LANES), f32)
    messages = pl.pallas_call(route_kernel, out_shape=[message] * 4, compiler_params=small, name="route")(
        blocks, incoming
    )
    messages = exchange(messages, "gz")
    piece = jax.ShapeDtypeStruct((PIECE, LANES), f32)
    pieces = pl.pallas_call(
        combine_kernel,
        out_shape=[piece] * 4,
        scratch_shapes=[pltpu.VMEM((4, BLOCK, LANES), f32)],
        compiler_params=small,
        name="combine",
    )(*messages)
    pieces = exchange(pieces, "gy")
    result = jax.ShapeDtypeStruct(troponin.shape, f32)
    return pl.pallas_call(
        tension_kernel,
        out_shape=[result, result],
        scratch_shapes=[pltpu.VMEM((4, PIECE, LANES), f32)],
        compiler_params=small,
        name="tension",
    )(*pieces, troponin, tension, unbind_rate, relax_rate)


def solution(mesh):
    node_spec = P("gx", ("gy", "gz"), None)
    return jax.shard_map(
        per_device,
        mesh=mesh,
        in_specs=(P(None, "gx", "gz", "gy"),) * 2 + (P(),) * 6 + (node_spec,) * 4,
        out_specs=(node_spec, node_spec),
        check_vma=False,
    )
```

profile of v0, /device:TPU:1, one launch (start us, length us, event | category | flops | bytes accessed | tf_op | source)
XLA Modules:
  0.0 27.0 jit_solution(6581769639154606580)
XLA Ops:
  0.6 0.0 copy-start.1
  0.7 2.3 %edge.1 = (f32[48,128]{1,0:T(8,128)S(1)}, f32[16,128]{1,0:T(8,128)S(1)}, f32[16,128]{1,0:T(8,128)S(1)}, bf16[512,256]{1,0:T(8,128)(2,1)S(1)}, bf16[512,256]{1,0:T(8,128)(2,1)S(1)}) custom-call(f32[8,32,32,128]{3,2,1,0:T(8,128)} %calcium.3, f32[8,32,32,128]{3,2,1,0:T(8,128)} %activation.3, s32[256]{0:T(256)} %element_first.1, f32[256]{0:T(256)} %offset_first.1, ...), custom_call_target="tpu_custom_call" | custom-call | tf_op jit(solution)/shard_map/edge/pallas_call | solution.py:383
  2.9 2.1 %collective-permute-start = (f32[48,128]{1,0:T(8,128)S(1)}, f32[48,128]{1,0:T(8,128)S(1)}, u32[]{:S(2)}, u32[]{:S(2)}) collective-permute-start(f32[48,128]{1,0:T(8,128)S(1)} %get-tuple-element.19), channel_id=1, source_target_pairs={{0,16},{16,32},{32,48},{48,64},{64,80},{80,96},{96,112},{112,0},{1... | collective-permute-start | bytes 73736 | tf_op jit(solution)/shard_map/ppermute | solution.py:405
  5.0 0.0 copy-done.1
  5.1 0.0 copy-start.4
  5.1 0.0 copy-start.5
  5.1 2.5 %restrict.1.blocks = f32[4,104,128]{2,1,0:T(8,128)S(1)} custom-call(f32[8,32,32,128]{3,2,1,0:T(8,128)S(1)} %copy-done, f32[8,32,32,128]{3,2,1,0:T(8,128)S(1)} %copy-done.1, f32[16,128]{1,0:T(8,128)S(1)} %get-tuple-element.15.first_weight, f32[16,128]{1,0:T(8,128)S(1)} %get-tuple-element.16.depth_weight, bf16[512,256]{1,0:T(8,128)(2,1)S(1)} %get-tuple-element.17.col_high, ...), custom_call_target="tpu_custom_call" | custom-call | tf_op jit(solution)/shard_map/restrict/pallas_call | solution.py:406
  7.6 3.2 %collective-permute-done.incoming = f32[48,128]{1,0:T(8,128)S(1)} collective-permute-done((f32[48,128]{1,0:T(8,128)S(1)}, f32[48,128]{1,0:T(8,128)S(1)}, u32[]{:S(2)}, u32[]{:S(2)}) %collective-permute-start) | collective-permute-done | bytes 24608 | tf_op jit(solution)/shard_map/ppermute | solution.py:405
  10.8 0.1 route.1
  10.9 1.4 %collective-permute-start.1 = (f32[104,128]{1,0:T(8,128)S(1)}, f32[104,128]{1,0:T(8,128)S(1)}, u32[]{:S(2)}, u32[]{:S(2)}) collective-permute-start(f32[104,128]{1,0:T(8,128)S(1)} %get-tuple-element.21), channel_id=1, source_target_pairs={{0,1},{1,2},{2,3},{3,0},{4,5},{5,6},{6,7},{7,4},{8,9},{9,10},{10,1... | collective-permute-start | bytes 159752 | tf_op jit(solution)/shard_map/ppermute | solution.py:352
  12.3 2.6 %collective-permute-start.2 = (f32[104,128]{1,0:T(8,128)S(1)}, f32[104,128]{1,0:T(8,128)S(1)}, u32[]{:S(2)}, u32[]{:S(2)}) collective-permute-start(f32[104,128]{1,0:T(8,128)S(1)} %get-tuple-element.22), channel_id=1, source_target_pairs={{0,2},{1,3},{2,0},{3,1},{4,6},{5,7},{6,4},{7,5},{8,10},{9,11},{10,... | collective-permute-start | bytes 159752 | tf_op jit(solution)/shard_map/ppermute | solution.py:352
  14.9 1.1 %collective-permute-start.3 = (f32[104,128]{1,0:T(8,128)S(1)}, f32[104,128]{1,0:T(8,128)S(1)}, u32[]{:S(2)}, u32[]{:S(2)}) collective-permute-start(f32[104,128]{1,0:T(8,128)S(1)} %get-tuple-element.23), channel_id=1, source_target_pairs={{0,3},{1,0},{2,1},{3,2},{4,7},{5,4},{6,5},{7,6},{8,11},{9,8},{10,9... | collective-permute-start | bytes 159752 | tf_op jit(solution)/shard_map/ppermute | solution.py:352
  16.0 0.0 collective-permute-done.1.one
  16.0 1.1 %collective-permute-done.2.two = f32[104,128]{1,0:T(8,128)S(1)} collective-permute-done((f32[104,128]{1,0:T(8,128)S(1)}, f32[104,128]{1,0:T(8,128)S(1)}, u32[]{:S(2)}, u32[]{:S(2)}) %collective-permute-start.2) | collective-permute-done | bytes 53280 | tf_op jit(solution)/shard_map/ppermute | solution.py:352
  17.0 1.6 %collective-permute-done.3.three = f32[104,128]{1,0:T(8,128)S(1)} collective-permute-done((f32[104,128]{1,0:T(8,128)S(1)}, f32[104,128]{1,0:T(8,128)S(1)}, u32[]{:S(2)}, u32[]{:S(2)}) %collective-permute-start.3) | collective-permute-done | bytes 53280 | tf_op jit(solution)/shard_map/ppermute | solution.py:352
  18.6 0.1 combine.1
  18.7 3.7 %collective-permute-start.4 = (f32[72,128]{1,0:T(8,128)S(1)}, f32[72,128]{1,0:T(8,128)S(1)}, u32[]{:S(2)}, u32[]{:S(2)}) collective-permute-start(f32[72,128]{1,0:T(8,128)S(1)} %get-tuple-element.25), channel_id=1, source_target_pairs={{0,4},{4,8},{8,12},{12,0},{1,5},{5,9},{9,13},{13,1},{2,6},{6,10},{... | collective-permute-start | bytes 110600 | tf_op jit(solution)/shard_map/ppermute | solution.py:352
  22.4 0.3 %collective-permute-start.5 = (f32[72,128]{1,0:T(8,128)S(1)}, f32[72,128]{1,0:T(8,128)S(1)}, u32[]{:S(2)}, u32[]{:S(2)}) collective-permute-start(f32[72,128]{1,0:T(8,128)S(1)} %get-tuple-element.26), channel_id=1, source_target_pairs={{0,8},{4,12},{8,0},{12,4},{1,9},{5,13},{9,1},{13,5},{2,10},{6,14},... | collective-permute-start | bytes 110600 | tf_op jit(solution)/shard_map/ppermute | solution.py:352
  22.6 0.2 collective-permute-start.6
  22.9 0.6 %collective-permute-done.4.one = f32[72,128]{1,0:T(8,128)S(1)} collective-permute-done((f32[72,128]{1,0:T(8,128)S(1)}, f32[72,128]{1,0:T(8,128)S(1)}, u32[]{:S(2)}, u32[]{:S(2)}) %collective-permute-start.4) | collective-permute-done | bytes 36896 | tf_op jit(solution)/shard_map/ppermute | solution.py:352
  23.4 1.7 %collective-permute-done.5.two = f32[72,128]{1,0:T(8,128)S(1)} collective-permute-done((f32[72,128]{1,0:T(8,128)S(1)}, f32[72,128]{1,0:T(8,128)S(1)}, u32[]{:S(2)}, u32[]{:S(2)}) %collective-permute-start.5) | collective-permute-done | bytes 36896 | tf_op jit(solution)/shard_map/ppermute | solution.py:352
  25.2 0.8 %collective-permute-done.6.three = f32[72,128]{1,0:T(8,128)S(1)} collective-permute-done((f32[72,128]{1,0:T(8,128)S(1)}, f32[72,128]{1,0:T(8,128)S(1)}, u32[]{:S(2)}, u32[]{:S(2)}) %collective-permute-start.6) | collective-permute-done | bytes 36896 | tf_op jit(solution)/shard_map/ppermute | solution.py:352
  26.0 0.0 copy-done.4
  26.0 0.9 %tension.2 = (f32[8,2,128]{2,1,0:T(2,128)}, f32[8,2,128]{2,1,0:T(2,128)}) custom-call(f32[72,128]{1,0:T(8,128)S(1)} %get-tuple-element.24.own, f32[72,128]{1,0:T(8,128)S(1)} %collective-permute-done.4.one, f32[72,128]{1,0:T(8,128)S(1)} %collective-permute-done.5.two, f32[72,128]{1,0:T(8,128)S(1)} %collective-permute-done.6.three, ...), custom_call_target="tpu_custom_call" | custom-call | tf_op jit(solution)/shard_map/tension/pallas_call | solution.py:429
  (7 shorter events, 0.0 us)
Async XLA Ops:
  0.6 4.4 %copy-start.1 = (f32[8,32,32,128]{3,2,1,0:T(8,128)S(1)}, f32[8,32,32,128]{3,2,1,0:T(8,128)}, u32[]{:S(2)}) copy-start(f32[8,32,32,128]{3,2,1,0:T(8,128)} %activation.3) | copy-start | bytes 12582916
  0.6 4.4 %copy-start = (f32[8,32,32,128]{3,2,1,0:T(8,128)S(1)}, f32[8,32,32,128]{3,2,1,0:T(8,128)}, u32[]{:S(2)}) copy-start(f32[8,32,32,128]{3,2,1,0:T(8,128)} %calcium.3) | copy-start | bytes 12582916
  2.9 7.9 %collective-permute-start = (f32[48,128]{1,0:T(8,128)S(1)}, f32[48,128]{1,0:T(8,128)S(1)}, u32[]{:S(2)}, u32[]{:S(2)}) collective-permute-start(f32[48,128]{1,0:T(8,128)S(1)} %get-tuple-element.19), channel_id=1, source_target_pairs={{0,16},{16,32},{32,48},{48,64},{64,80},{80,96},{96,112},{112,0},{1... | collective-permute-start | bytes 73736 | tf_op jit(solution)/shard_map/ppermute | solution.py:405
  5.1 21.0 %copy-start.2 = (f32[8,2,128]{2,1,0:T(2,128)S(1)}, f32[8,2,128]{2,1,0:T(2,128)}, u32[]{:S(2)}) copy-start(f32[8,2,128]{2,1,0:T(2,128)} %troponin.1) | copy-start | bytes 24580
  5.1 21.0 %copy-start.3 = (f32[8,2,128]{2,1,0:T(2,128)S(1)}, f32[8,2,128]{2,1,0:T(2,128)}, u32[]{:S(2)}) copy-start(f32[8,2,128]{2,1,0:T(2,128)} %tension.3) | copy-start | bytes 24580
  5.1 21.0 %copy-start.4 = (f32[8,2,128]{2,1,0:T(2,128)S(1)}, f32[8,2,128]{2,1,0:T(2,128)}, u32[]{:S(2)}) copy-start(f32[8,2,128]{2,1,0:T(2,128)} %unbind.1) | copy-start | bytes 24580
  5.1 21.0 %copy-start.5 = (f32[8,2,128]{2,1,0:T(2,128)S(1)}, f32[8,2,128]{2,1,0:T(2,128)}, u32[]{:S(2)}) copy-start(f32[8,2,128]{2,1,0:T(2,128)} %relax.1) | copy-start | bytes 24580
  10.9 5.0 %collective-permute-start.1 = (f32[104,128]{1,0:T(8,128)S(1)}, f32[104,128]{1,0:T(8,128)S(1)}, u32[]{:S(2)}, u32[]{:S(2)}) collective-permute-start(f32[104,128]{1,0:T(8,128)S(1)} %get-tuple-element.21), channel_id=1, source_target_pairs={{0,1},{1,2},{2,3},{3,0},{4,5},{5,6},{6,7},{7,4},{8,9},{9,10},{10,1... | collective-permute-start | bytes 159752 | tf_op jit(solution)/shard_map/ppermute | solution.py:352
  12.3 4.7 %collective-permute-start.2 = (f32[104,128]{1,0:T(8,128)S(1)}, f32[104,128]{1,0:T(8,128)S(1)}, u32[]{:S(2)}, u32[]{:S(2)}) collective-permute-start(f32[104,128]{1,0:T(8,128)S(1)} %get-tuple-element.22), channel_id=1, source_target_pairs={{0,2},{1,3},{2,0},{3,1},{4,6},{5,7},{6,4},{7,5},{8,10},{9,11},{10,... | collective-permute-start | bytes 159752 | tf_op jit(solution)/shard_map/ppermute | solution.py:352
  14.9 3.7 %collective-permute-start.3 = (f32[104,128]{1,0:T(8,128)S(1)}, f32[104,128]{1,0:T(8,128)S(1)}, u32[]{:S(2)}, u32[]{:S(2)}) collective-permute-start(f32[104,128]{1,0:T(8,128)S(1)} %get-tuple-element.23), channel_id=1, source_target_pairs={{0,3},{1,0},{2,1},{3,2},{4,7},{5,4},{6,5},{7,6},{8,11},{9,8},{10,9... | collective-permute-start | bytes 159752 | tf_op jit(solution)/shard_map/ppermute | solution.py:352
  18.7 4.7 %collective-permute-start.4 = (f32[72,128]{1,0:T(8,128)S(1)}, f32[72,128]{1,0:T(8,128)S(1)}, u32[]{:S(2)}, u32[]{:S(2)}) collective-permute-start(f32[72,128]{1,0:T(8,128)S(1)} %get-tuple-element.25), channel_id=1, source_target_pairs={{0,4},{4,8},{8,12},{12,0},{1,5},{5,9},{9,13},{13,1},{2,6},{6,10},{... | collective-permute-start | bytes 110600 | tf_op jit(solution)/shard_map/ppermute | solution.py:352
  22.4 2.8 %collective-permute-start.5 = (f32[72,128]{1,0:T(8,128)S(1)}, f32[72,128]{1,0:T(8,128)S(1)}, u32[]{:S(2)}, u32[]{:S(2)}) collective-permute-start(f32[72,128]{1,0:T(8,128)S(1)} %get-tuple-element.26), channel_id=1, source_target_pairs={{0,8},{4,12},{8,0},{12,4},{1,9},{5,13},{9,1},{13,5},{2,10},{6,14},... | collective-permute-start | bytes 110600 | tf_op jit(solution)/shard_map/ppermute | solution.py:352
  22.6 3.4 %collective-permute-start.6 = (f32[72,128]{1,0:T(8,128)S(1)}, f32[72,128]{1,0:T(8,128)S(1)}, u32[]{:S(2)}, u32[]{:S(2)}) collective-permute-start(f32[72,128]{1,0:T(8,128)S(1)} %get-tuple-element.27), channel_id=1, source_target_pairs={{0,12},{4,0},{8,4},{12,8},{1,13},{5,1},{9,5},{13,9},{2,14},{6,2},{... | collective-permute-start | bytes 110600 | tf_op jit(solution)/shard_map/ppermute | solution.py:352
where the time goes:
time: 27.1 us; the launch traced here: 27 us
  starting transfers between devices  11.3 us (42%)
  waiting for transfers between devices  8.99 us (33%)
  Pallas kernels  5.94 us (22%)
  between operations  0.7 us (3%)
    ppermute x6, starting transfers between devices, exchange(): received[k] = lax.ppermute(messages[k], axis, pairs)  9.19 us
    ppermute x6, waiting for transfers between devices, exchange(): received[k] = lax.ppermute(messages[k], axis, pairs)  5.78 us
    ppermute x1, waiting for transfers between devices, per_device(): incoming = lax.ppermute(edge, 'gx', [(i, (i + 1) % 8) for i in range(8)])  3.21 us
    pallas_call x1, Pallas kernels, per_device(): pl.pallas_call(restrict_kernel, out_shape=jax.ShapeDtypeStruct((4, BLOCK,...  2.55 us
    pallas_call x1, Pallas kernels, per_device(): pl.pallas_call(edge_kernel, in_specs=[pl.BlockSpec(memory_space=pltpu.HBM...  2.28 us
    ppermute x1, starting transfers between devices, per_device(): incoming = lax.ppermute(edge, 'gx', [(i, (i + 1) % 8) for i in range(8)])  2.1 us
    pallas_call x1, Pallas kernels, per_device(): pl.pallas_call(tension_kernel, out_shape=[result, result], scratch_shapes...  0.9 us
  transfers between devices with their start and end apart: 7, of which 6 were waited for; matrix products, arithmetic and copies ran while one was open for 0% of the time, Pallas kernels for 9%

commit v1 on v0

--- a/solution.py
+++ b/solution.py
@@ -19,7 +19,7 @@
 COLS = 32
 ROWS = 72
 BLOCK = 104
-SURE = 28
+SURE = 26
 PIECE = 72
 
 
@@ -37,6 +37,10 @@
 def halves(value):
     high = value.astype(bf16).astype(f32)
     return high, value - high
+
+
+def plane_row(j, p):
+    return j * 16 + p * 8 if p < 2 else PIECE + j * 8
 
 
 def lane_ids(rows):
@@ -96,7 +100,15 @@
         load.start()
     for copy in sure_copies:
         copy.start()
-    loads[0].wait()
+    for load in loads[:4]:
+        load.wait()
+
+    first = hat(elements_1[...], offsets_1[...], gx * NODES, 16)
+    own = jnp.where(gx >= 4, first[:, LANES:], first[:, :LANES])
+    third = hat(elements_3[...], offsets_3[...], gz * NODES, 16)
+    depth = pick_lanes(third, gz * 32 + lane_ids(16) % 32)
+    first_weight[...] = own
+    depth_weight[...] = depth
 
     place = lax.broadcasted_iota(jnp.int32, (1, 256), 1)
     earlier = jnp.logical_and(
@@ -115,17 +127,6 @@
         return carry
 
     lax.fori_loop(0, count, start, 0)
-    loads[1].wait()
-    loads[2].wait()
-    loads[3].wait()
-
-    first = hat(elements_1[...], offsets_1[...], gx * NODES, 16)
-    own = jnp.where(gx >= 4, first[:, LANES:], first[:, :LANES])
-    third = hat(elements_3[...], offsets_3[...], gz * NODES, 16)
-    depth = pick_lanes(third, gz * 32 + lane_ids(16) % 32)
-    first_weight[...] = own
-    depth_weight[...] = depth
-
     loads[4].wait()
     loads[5].wait()
     second = hat(elements_2[...], offsets_2[...], gy * COLS, 40)
@@ -240,12 +241,12 @@
         for p, plane in enumerate((2 * k, 2 * k + 1, NODES)):
             rows = slice(plane * 8, plane * 8 + 8)
             for j in range(4):
-                start = j * 24 + p * 8
+                start = plane_row(j, p)
                 blocks[k, start : start + 8] = main[j][rows]
             piece = extra[rows]
             piece = piece if p == 0 else pltpu.roll(piece, 4 * p, 1)
             tail = piece if tail is None else tail + piece
-        blocks[k, 96:104] = tail
+        blocks[k, 64:72] = tail
 
 
 def route_kernel(blocks, incoming, *outs):
@@ -258,14 +259,14 @@
         tail = None
         for p in range(3):
             for j in range(4):
-                start = j * 24 + p * 8
+                start = plane_row(j, p)
                 if p < 2:
                     row = incoming[pl.ds(j * 8 + 2 * which + p, 1), :]
                 else:
                     row = incoming[32 + j : 33 + j, :]
-                out[start : start + 8] = blocks[which, start : start + 8] + jnp.where(
-                    top, row, 0.0
-                )
+                if start < out.shape[0]:
+                    own = blocks[which, start : start + 8]
+                    out[start : start + 8] = own + jnp.where(top, row, 0.0)
             if p < 2:
                 row = incoming[pl.ds(40 + 2 * which + p, 1), :]
             else:
@@ -273,14 +274,14 @@
             row = jnp.where(top, row, 0.0)
             row = row if p == 0 else pltpu.roll(row, 4 * p, 1)
             tail = row if tail is None else tail + row
-        out[96:104] = blocks[which, 96:104] + tail
+        out[64:72] = blocks[which, 64:72] + tail
 
 
 def combine_kernel(own, one, two, three, *rest):
     outs, slabs = rest[:4], rest[4]
     gy, gz = lax.axis_index("gy"), lax.axis_index("gz")
     for k, message in enumerate((own, one, two, three)):
-        slabs[lax.rem(gz + 4 - k, 4)] = message[...]
+        slabs[lax.rem(gz + 4 - k, 4), : message.shape[0]] = message[...]
     lane = lane_ids(8)
     for k in range(4):
         slab = lax.rem(gy + k, 4)
@@ -288,15 +289,15 @@
         joins = jnp.logical_and(gz == 0, slab > 0)
         out = outs[k]
         for j in range(4):
-            start = j * 24
-            plane = slabs[before, start + 16 : start + 24]
-            out[j * 16 : j * 16 + 8] = slabs[slab, start : start + 8] + jnp.where(
-                joins, plane, 0.0
-            )
-            out[j * 16 + 8 : j * 16 + 16] = slabs[slab, start + 8 : start + 16]
-        tail = pltpu.roll(slabs[before, 96:104], LANES - 8, 1)
+            start = plane_row(j, 0)
+            plane = slabs[before, plane_row(j, 2) : plane_row(j, 2) + 8]
+            own = slabs[slab, start : start + 8]
+            out[start : start + 8] = own + jnp.where(joins, plane, 0.0)
+            start = plane_row(j, 1)
+            out[start : start + 8] = slabs[slab, start : start + 8]
+        tail = pltpu.roll(slabs[before, 64:72], LANES - 8, 1)
         tail = jnp.where(jnp.logical_and(joins, lane % COLS < 4), tail, 0.0)
-        out[64:72] = slabs[slab, 96:104] + tail
+        out[64:72] = slabs[slab, 64:72] + tail
 
 
 def tension_kernel(
@@ -306,25 +307,44 @@
     for k, message in enumerate((own, one, two, three)):
         chunks[lax.rem(gy + 4 - k, 4)] = message[...]
     lane = lane_ids(8)
-    pieces = [chunks[c] for c in range(4)]
+    quarter = lane // COLS
+    odd = quarter % 2 == 1
+    upper = quarter >= 2
 
     def turn(value, shift):
         shift = shift % LANES
         return value if shift == 0 else pltpu.roll(value, shift, 1)
 
+    def spread(start):
+        v = [chunks[c, start : start + 8] for c in range(4)]
+        low = [jnp.where(upper, turn(v[c + 2], 64), v[c]) for c in range(2)]
+        high = [jnp.where(upper, v[c + 2], turn(v[c], 64)) for c in range(2)]
+        out = []
+        for one, two in (low, high):
+            out.append(jnp.where(odd, turn(two, COLS), one))
+            out.append(jnp.where(odd, two, turn(one, -COLS)))
+        return out
+
+    def ends(group):
+        total = None
+        for c in range(3):
+            part = turn(chunks[c, 64:72], COLS * (c + 1 - group))
+            part = jnp.where(quarter == c + 1, part, 0.0)
+            total = part if total is None else total + part
+        return total
+
+    starts = lane % COLS == 0
+    last_columns = [ends(group) for group in range(4)]
+    drives = {}
+    for plane in range(2):
+        for j in range(4):
+            for group, value in enumerate(spread(j * 16 + plane * 8)):
+                extra = turn(last_columns[group], -(4 * plane + j))
+                value = value + jnp.where(starts, extra, 0.0)
+                drives[j // 2, 4 * (j % 2) + group, plane] = value
+
     def drive(f, substep, plane):
-        half, group = divmod(substep, 4)
-        j = 2 * f + half
-        start = j * 16 + plane * 8
-        total = None
-        for c in range(4):
-            part = turn(pieces[c][start : start + 8], COLS * (c - group))
-            total = part if total is None else jnp.where(lane // COLS == c, part, total)
-        for c in range(3):
-            shift = COLS * (c + 1) - (COLS * group + 4 * plane + j)
-            part = turn(pieces[c][64:72], shift)
-            total = total + jnp.where(lane == COLS * (c + 1), part, 0.0)
-        return total
+        return drives[f, substep, plane]
 
     for plane in range(2):
         bound = troponin[:, plane, :]
@@ -411,8 +431,9 @@
         name="restrict",
     )(calcium, activation, *weights)
     small = pltpu.CompilerParams(vmem_limit_bytes=4 << 20)
-    message = jax.ShapeDtypeStruct((BLOCK, LANES), f32)
-    messages = pl.pallas_call(route_kernel, out_shape=[message] * 4, compiler_params=small, name="route")(
+    sizes = [PIECE if k == 1 else BLOCK for k in range(4)]
+    message = [jax.ShapeDtypeStruct((n, LANES), f32) for n in sizes]
+    messages = pl.pallas_call(route_kernel, out_shape=message, compiler_params=small, name="route")(
         blocks, incoming
     )
     messages = exchange(messages, "gz")

time: 27.1 us -> 28 us (1.033)
  waiting for transfers between devices: 8.99 us -> 9.7 us
    ppermute x6, waiting for transfers between devices: 5.78 us -> 6.49 us  [exchange(): received[k] = lax.ppermute(messages[k], axis, pairs)]
  transfers between devices with their start and end apart: 7 -> 7, of which waited for: 6 -> 5; matrix products, arithmetic and copies ran while one was open for 0% -> 0% of each run, Pallas kernels for 9% -> 9%
where the time goes in v1:
time: 28 us; the launch traced here: 27.9 us
  starting transfers between devices  11.4 us (41%)
  waiting for transfers between devices  9.7 us (35%)
  Pallas kernels  6.03 us (22%)
  between operations  0.7 us (2%)
    ppermute x6, starting transfers between devices, exchange(): received[k] = lax.ppermute(messages[k], axis, pairs)  9.3 us
    ppermute x6, waiting for transfers between devices, exchange(): received[k] = lax.ppermute(messages[k], axis, pairs)  6.49 us
    ppermute x1, waiting for transfers between devices, per_device(): incoming = lax.ppermute(edge, 'gx', [(i, (i + 1) % 8) for i in range(8)])  3.21 us
    pallas_call x1, Pallas kernels, per_device(): pl.pallas_call(restrict_kernel, out_shape=jax.ShapeDtypeStruct((4, BLOCK,...  2.55 us
    pallas_call x1, Pallas kernels, per_device(): pl.pallas_call(edge_kernel, in_specs=[pl.BlockSpec(memory_space=pltpu.HBM...  2.44 us
    ppermute x1, starting transfers between devices, per_device(): incoming = lax.ppermute(edge, 'gx', [(i, (i + 1) % 8) for i in range(8)])  2.1 us
    pallas_call x1, Pallas kernels, per_device(): pl.pallas_call(tension_kernel, out_shape=[result, result], scratch_shapes...  0.85 us
  transfers between devices with their start and end apart: 7, of which 5 were waited for; matrix products, arithmetic and copies ran while one was open for 0% of the time, Pallas kernels for 9%

profile of v1, /device:TPU:1, one launch (start us, length us, event | category | flops | bytes accessed | tf_op | source)
XLA Modules:
  0.0 27.9 jit_solution(4540600890433777928)
XLA Ops:
  0.6 0.0 copy-start.1
  0.7 2.4 %edge.1 = (f32[48,128]{1,0:T(8,128)S(1)}, f32[16,128]{1,0:T(8,128)S(1)}, f32[16,128]{1,0:T(8,128)S(1)}, bf16[512,256]{1,0:T(8,128)(2,1)S(1)}, bf16[512,256]{1,0:T(8,128)(2,1)S(1)}) custom-call(f32[8,32,32,128]{3,2,1,0:T(8,128)} %calcium.3, f32[8,32,32,128]{3,2,1,0:T(8,128)} %activation.3, s32[256]{0:T(256)} %element_first.1, f32[256]{0:T(256)} %offset_first.1, ...), custom_call_target="tpu_custom_call" | custom-call | tf_op jit(solution)/shard_map/edge/pallas_call | solution.py:403
  3.1 2.1 %collective-permute-start = (f32[48,128]{1,0:T(8,128)S(1)}, f32[48,128]{1,0:T(8,128)S(1)}, u32[]{:S(2)}, u32[]{:S(2)}) collective-permute-start(f32[48,128]{1,0:T(8,128)S(1)} %get-tuple-element.19), channel_id=1, source_target_pairs={{0,16},{16,32},{32,48},{48,64},{64,80},{80,96},{96,112},{112,0},{1... | collective-permute-start | bytes 73736 | tf_op jit(solution)/shard_map/ppermute | solution.py:425
  5.2 0.0 copy-start.4
  5.2 0.0 copy-start.5
  5.2 2.5 %restrict.1.blocks = f32[4,104,128]{2,1,0:T(8,128)S(1)} custom-call(f32[8,32,32,128]{3,2,1,0:T(8,128)S(1)} %copy-done, f32[8,32,32,128]{3,2,1,0:T(8,128)S(1)} %copy-done.1, f32[16,128]{1,0:T(8,128)S(1)} %get-tuple-element.15.first_weight, f32[16,128]{1,0:T(8,128)S(1)} %get-tuple-element.16.depth_weight, bf16[512,256]{1,0:T(8,128)(2,1)S(1)} %get-tuple-element.17.col_high, ...), custom_call_target="tpu_custom_call" | custom-call | tf_op jit(solution)/shard_map/restrict/pallas_call | solution.py:426
  7.8 3.2 %collective-permute-done.incoming = f32[48,128]{1,0:T(8,128)S(1)} collective-permute-done((f32[48,128]{1,0:T(8,128)S(1)}, f32[48,128]{1,0:T(8,128)S(1)}, u32[]{:S(2)}, u32[]{:S(2)}) %collective-permute-start) | collective-permute-done | bytes 24608 | tf_op jit(solution)/shard_map/ppermute | solution.py:425
  11.0 0.1 route.1
  11.1 3.0 %collective-permute-start.2 = (f32[104,128]{1,0:T(8,128)S(1)}, f32[104,128]{1,0:T(8,128)S(1)}, u32[]{:S(2)}, u32[]{:S(2)}) collective-permute-start(f32[104,128]{1,0:T(8,128)S(1)} %get-tuple-element.22), channel_id=1, source_target_pairs={{0,2},{1,3},{2,0},{3,1},{4,6},{5,7},{6,4},{7,5},{8,10},{9,11},{10,... | collective-permute-start | bytes 159752 | tf_op jit(solution)/shard_map/ppermute | solution.py:372
  14.1 0.8 %collective-permute-start.3 = (f32[104,128]{1,0:T(8,128)S(1)}, f32[104,128]{1,0:T(8,128)S(1)}, u32[]{:S(2)}, u32[]{:S(2)}) collective-permute-start(f32[104,128]{1,0:T(8,128)S(1)} %get-tuple-element.23), channel_id=1, source_target_pairs={{0,3},{1,0},{2,1},{3,2},{4,7},{5,4},{6,5},{7,6},{8,11},{9,8},{10,9... | collective-permute-start | bytes 159752 | tf_op jit(solution)/shard_map/ppermute | solution.py:372
  14.8 0.7 %collective-permute-start.1 = (f32[72,128]{1,0:T(8,128)S(1)}, f32[72,128]{1,0:T(8,128)S(1)}, u32[]{:S(2)}, u32[]{:S(2)}) collective-permute-start(f32[72,128]{1,0:T(8,128)S(1)} %get-tuple-element.21), channel_id=1, source_target_pairs={{0,1},{1,2},{2,3},{3,0},{4,5},{5,6},{6,7},{7,4},{8,9},{9,10},{10,1... | collective-permute-start | bytes 110600 | tf_op jit(solution)/shard_map/ppermute | solution.py:372
  15.5 3.3 %collective-permute-done.1.one = f32[72,128]{1,0:T(8,128)S(1)} collective-permute-done((f32[72,128]{1,0:T(8,128)S(1)}, f32[72,128]{1,0:T(8,128)S(1)}, u32[]{:S(2)}, u32[]{:S(2)}) %collective-permute-start.1) | collective-permute-done | bytes 36896 | tf_op jit(solution)/shard_map/ppermute | solution.py:372
  18.9 0.0 collective-permute-done.2.two
  18.9 0.0 collective-permute-done.3.three
  18.9 0.1 combine.1
  19.0 4.4 %collective-permute-start.4 = (f32[72,128]{1,0:T(8,128)S(1)}, f32[72,128]{1,0:T(8,128)S(1)}, u32[]{:S(2)}, u32[]{:S(2)}) collective-permute-start(f32[72,128]{1,0:T(8,128)S(1)} %get-tuple-element.25), channel_id=1, source_target_pairs={{0,4},{4,8},{8,12},{12,0},{1,5},{5,9},{9,13},{13,1},{2,6},{6,10},{... | collective-permute-start | bytes 110600 | tf_op jit(solution)/shard_map/ppermute | solution.py:372
  23.3 0.3 collective-permute-start.5
  23.6 0.2 collective-permute-start.6
  23.8 0.6 %collective-permute-done.4.one = f32[72,128]{1,0:T(8,128)S(1)} collective-permute-done((f32[72,128]{1,0:T(8,128)S(1)}, f32[72,128]{1,0:T(8,128)S(1)}, u32[]{:S(2)}, u32[]{:S(2)}) %collective-permute-start.4) | collective-permute-done | bytes 36896 | tf_op jit(solution)/shard_map/ppermute | solution.py:372
  24.4 1.7 %collective-permute-done.5.two = f32[72,128]{1,0:T(8,128)S(1)} collective-permute-done((f32[72,128]{1,0:T(8,128)S(1)}, f32[72,128]{1,0:T(8,128)S(1)}, u32[]{:S(2)}, u32[]{:S(2)}) %collective-permute-start.5) | collective-permute-done | bytes 36896 | tf_op jit(solution)/shard_map/ppermute | solution.py:372
  26.2 0.8 %collective-permute-done.6.three = f32[72,128]{1,0:T(8,128)S(1)} collective-permute-done((f32[72,128]{1,0:T(8,128)S(1)}, f32[72,128]{1,0:T(8,128)S(1)}, u32[]{:S(2)}, u32[]{:S(2)}) %collective-permute-start.6) | collective-permute-done | bytes 36896 | tf_op jit(solution)/shard_map/ppermute | solution.py:372
  27.0 0.0 copy-done.2
  27.0 0.0 copy-done.4
  27.0 0.8 %tension.2 = (f32[8,2,128]{2,1,0:T(2,128)}, f32[8,2,128]{2,1,0:T(2,128)}) custom-call(f32[72,128]{1,0:T(8,128)S(1)} %get-tuple-element.24.own, f32[72,128]{1,0:T(8,128)S(1)} %collective-permute-done.4.one, f32[72,128]{1,0:T(8,128)S(1)} %collective-permute-done.5.two, f32[72,128]{1,0:T(8,128)S(1)} %collective-permute-done.6.three, ...), custom_call_target="tpu_custom_call" | custom-call | tf_op jit(solution)/shard_map/tension/pallas_call | solution.py:450
  (7 shorter events, 0.0 us)
Async XLA Ops:
  0.6 4.6 %copy-start.1 = (f32[8,32,32,128]{3,2,1,0:T(8,128)S(1)}, f32[8,32,32,128]{3,2,1,0:T(8,128)}, u32[]{:S(2)}) copy-start(f32[8,32,32,128]{3,2,1,0:T(8,128)} %activation.3) | copy-start | bytes 12582916
  0.6 4.6 %copy-start = (f32[8,32,32,128]{3,2,1,0:T(8,128)S(1)}, f32[8,32,32,128]{3,2,1,0:T(8,128)}, u32[]{:S(2)}) copy-start(f32[8,32,32,128]{3,2,1,0:T(8,128)} %calcium.3) | copy-start | bytes 12582916
  3.1 7.9 %collective-permute-start = (f32[48,128]{1,0:T(8,128)S(1)}, f32[48,128]{1,0:T(8,128)S(1)}, u32[]{:S(2)}, u32[]{:S(2)}) collective-permute-start(f32[48,128]{1,0:T(8,128)S(1)} %get-tuple-element.19), channel_id=1, source_target_pairs={{0,16},{16,32},{32,48},{48,64},{64,80},{80,96},{96,112},{112,0},{1... | collective-permute-start | bytes 73736 | tf_op jit(solution)/shard_map/ppermute | solution.py:425
  5.2 21.8 %copy-start.2 = (f32[8,2,128]{2,1,0:T(2,128)S(1)}, f32[8,2,128]{2,1,0:T(2,128)}, u32[]{:S(2)}) copy-start(f32[8,2,128]{2,1,0:T(2,128)} %troponin.1) | copy-start | bytes 24580
  5.2 21.8 %copy-start.3 = (f32[8,2,128]{2,1,0:T(2,128)S(1)}, f32[8,2,128]{2,1,0:T(2,128)}, u32[]{:S(2)}) copy-start(f32[8,2,128]{2,1,0:T(2,128)} %tension.3) | copy-start | bytes 24580
  5.2 21.8 %copy-start.4 = (f32[8,2,128]{2,1,0:T(2,128)S(1)}, f32[8,2,128]{2,1,0:T(2,128)}, u32[]{:S(2)}) copy-start(f32[8,2,128]{2,1,0:T(2,128)} %unbind.1) | copy-start | bytes 24580
  5.2 21.8 %copy-start.5 = (f32[8,2,128]{2,1,0:T(2,128)S(1)}, f32[8,2,128]{2,1,0:T(2,128)}, u32[]{:S(2)}) copy-start(f32[8,2,128]{2,1,0:T(2,128)} %relax.1) | copy-start | bytes 24580
  11.1 7.8 %collective-permute-start.2 = (f32[104,128]{1,0:T(8,128)S(1)}, f32[104,128]{1,0:T(8,128)S(1)}, u32[]{:S(2)}, u32[]{:S(2)}) collective-permute-start(f32[104,128]{1,0:T(8,128)S(1)} %get-tuple-element.22), channel_id=1, source_target_pairs={{0,2},{1,3},{2,0},{3,1},{4,6},{5,7},{6,4},{7,5},{8,10},{9,11},{10,... | collective-permute-start | bytes 159752 | tf_op jit(solution)/shard_map/ppermute | solution.py:372
  14.1 4.8 %collective-permute-start.3 = (f32[104,128]{1,0:T(8,128)S(1)}, f32[104,128]{1,0:T(8,128)S(1)}, u32[]{:S(2)}, u32[]{:S(2)}) collective-permute-start(f32[104,128]{1,0:T(8,128)S(1)} %get-tuple-element.23), channel_id=1, source_target_pairs={{0,3},{1,0},{2,1},{3,2},{4,7},{5,4},{6,5},{7,6},{8,11},{9,8},{10,9... | collective-permute-start | bytes 159752 | tf_op jit(solution)/shard_map/ppermute | solution.py:372
  14.8 4.0 %collective-permute-start.1 = (f32[72,128]{1,0:T(8,128)S(1)}, f32[72,128]{1,0:T(8,128)S(1)}, u32[]{:S(2)}, u32[]{:S(2)}) collective-permute-start(f32[72,128]{1,0:T(8,128)S(1)} %get-tuple-element.21), channel_id=1, source_target_pairs={{0,1},{1,2},{2,3},{3,0},{4,5},{5,6},{6,7},{7,4},{8,9},{9,10},{10,1... | collective-permute-start | bytes 110600 | tf_op jit(solution)/shard_map/ppermute | solution.py:372
  19.0 5.4 %collective-permute-start.4 = (f32[72,128]{1,0:T(8,128)S(1)}, f32[72,128]{1,0:T(8,128)S(1)}, u32[]{:S(2)}, u32[]{:S(2)}) collective-permute-start(f32[72,128]{1,0:T(8,128)S(1)} %get-tuple-element.25), channel_id=1, source_target_pairs={{0,4},{4,8},{8,12},{12,0},{1,5},{5,9},{9,13},{13,1},{2,6},{6,10},{... | collective-permute-start | bytes 110600 | tf_op jit(solution)/shard_map/ppermute | solution.py:372
  23.3 2.8 %collective-permute-start.5 = (f32[72,128]{1,0:T(8,128)S(1)}, f32[72,128]{1,0:T(8,128)S(1)}, u32[]{:S(2)}, u32[]{:S(2)}) collective-permute-start(f32[72,128]{1,0:T(8,128)S(1)} %get-tuple-element.26), channel_id=1, source_target_pairs={{0,8},{4,12},{8,0},{12,4},{1,9},{5,13},{9,1},{13,5},{2,10},{6,14},... | collective-permute-start | bytes 110600 | tf_op jit(solution)/shard_map/ppermute | solution.py:372
  23.6 3.4 %collective-permute-start.6 = (f32[72,128]{1,0:T(8,128)S(1)}, f32[72,128]{1,0:T(8,128)S(1)}, u32[]{:S(2)}, u32[]{:S(2)}) collective-permute-start(f32[72,128]{1,0:T(8,128)S(1)} %get-tuple-element.27), channel_id=1, source_target_pairs={{0,12},{4,0},{8,4},{12,8},{1,13},{5,1},{9,5},{13,9},{2,14},{6,2},{... | collective-permute-start | bytes 110600 | tf_op jit(solution)/shard_map/ppermute | solution.py:372

commit v2 on v1

--- a/solution.py
+++ b/solution.py
@@ -98,8 +98,13 @@
     ]
     for load in loads:
         load.start()
-    for copy in sure_copies:
-        copy.start()
+    passes_on = gx < 7
+
+    @pl.when(passes_on)
+    def _():
+        for copy in sure_copies:
+            copy.start()
+
     for load in loads[:4]:
         load.wait()
 
@@ -116,7 +121,7 @@
     )
     begin = jnp.sum(jnp.where(earlier, 1.0, 0.0)).astype(jnp.int32)
 
-    count = (SURE + 1 - begin) // 2
+    count = jnp.where(passes_on, (SURE + 1 - begin) // 2, 0)
 
     def start(n, carry):
         for f, field in enumerate(fields):
@@ -148,49 +153,51 @@
         col_high[rows] = high.astype(bf16)
         col_low[rows] = low.astype(bf16)
 
-    layer = jnp.broadcast_to(own[NODES : NODES + 1], (8, LANES))
-
-    def cell_weight(x):
-        index = jnp.full((8, LANES), lax.rem(gx, 4) * 32 + x, jnp.int32)
-        return jnp.concatenate([pick_lanes(layer, index)] * 4, 0)
-
-    slots = [(f, t, (f * SUBS + t) * LANES) for f in range(2) for t in range(SUBS)]
-    pltpu.make_async_copy(sure_cells, sure_cells, sure_sem).wait()
-    sure_weights = [cell_weight(x) for x in range(SURE, 32)]
-    for f, t, column in slots:
-        total = None
-        for n, weight in enumerate(sure_weights):
-            part = weight * sure_cells[f, t, n]
-            total = part if total is None else total + part
-        sums[:, column : column + LANES] = total
-
-    def add(n, carry):
-        pltpu.make_async_copy(cells.at[n], cells.at[n], cell_sems.at[n]).wait()
-        pair = [cell_weight(SURE - 2 - 2 * n + i) for i in range(2)]
+    @pl.when(passes_on)
+    def _():
+        layer = jnp.broadcast_to(own[NODES : NODES + 1], (8, LANES))
+
+        def cell_weight(x):
+            index = jnp.full((8, LANES), lax.rem(gx, 4) * 32 + x, jnp.int32)
+            return jnp.concatenate([pick_lanes(layer, index)] * 4, 0)
+
+        slots = [(f, t, (f * SUBS + t) * LANES) for f in range(2) for t in range(SUBS)]
+        pltpu.make_async_copy(sure_cells, sure_cells, sure_sem).wait()
+        sure_weights = [cell_weight(x) for x in range(SURE, 32)]
         for f, t, column in slots:
-            part = pair[0] * cells[n, f, t, 0] + pair[1] * cells[n, f, t, 1]
-            sums[:, column : column + LANES] += part
-        return carry
-
-    lax.fori_loop(0, count, add, 0)
-
-    depth_high, depth_low = halves(depth[:, :32])
-    weights = jnp.concatenate([depth_high, depth_low], 0).astype(bf16)
-    high, low = halves(sums[...])
-    upper = jnp.dot(weights, high.astype(bf16), preferred_element_type=f32)
-    lower = jnp.dot(weights[:16], low.astype(bf16), preferred_element_type=f32)
-    planes = upper[:16] + upper[16:] + lower
-    whole = jnp.concatenate([planes[:, j * 512 : (j + 1) * 512] for j in range(4)], 0)
-    result = columns(whole, col_high, col_low)
-    quads = [result[j * 16 : j * 16 + 16] for j in range(4)]
-    extra = quads[0][:, LANES:]
-    for j in range(1, 4):
-        extra = extra + pltpu.roll(quads[j][:, LANES:], j, 1)
-    for j in range(4):
-        edge[j * 8 : j * 8 + 8] = quads[j][:8, :LANES]
-    corners = [q[8:9, :LANES] for q in quads] + [extra[8:9]]
-    edge[32:40] = jnp.concatenate(corners + [jnp.zeros((3, LANES), f32)], 0)
-    edge[40:48] = extra[:8]
+            total = None
+            for n, weight in enumerate(sure_weights):
+                part = weight * sure_cells[f, t, n]
+                total = part if total is None else total + part
+            sums[:, column : column + LANES] = total
+
+        def add(n, carry):
+            pltpu.make_async_copy(cells.at[n], cells.at[n], cell_sems.at[n]).wait()
+            pair = [cell_weight(SURE - 2 - 2 * n + i) for i in range(2)]
+            for f, t, column in slots:
+                part = pair[0] * cells[n, f, t, 0] + pair[1] * cells[n, f, t, 1]
+                sums[:, column : column + LANES] += part
+            return carry
+
+        lax.fori_loop(0, count, add, 0)
+
+        depth_high, depth_low = halves(depth[:, :32])
+        weights = jnp.concatenate([depth_high, depth_low], 0).astype(bf16)
+        high, low = halves(sums[...])
+        upper = jnp.dot(weights, high.astype(bf16), preferred_element_type=f32)
+        lower = jnp.dot(weights[:16], low.astype(bf16), preferred_element_type=f32)
+        planes = upper[:16] + upper[16:] + lower
+        whole = jnp.concatenate([planes[:, j * 512 : (j + 1) * 512] for j in range(4)], 0)
+        result = columns(whole, col_high, col_low)
+        quads = [result[j * 16 : j * 16 + 16] for j in range(4)]
+        extra = quads[0][:, LANES:]
+        for j in range(1, 4):
+            extra = extra + pltpu.roll(quads[j][:, LANES:], j, 1)
+        for j in range(4):
+            edge[j * 8 : j * 8 + 8] = quads[j][:8, :LANES]
+        corners = [q[8:9, :LANES] for q in quads] + [extra[8:9]]
+        edge[32:40] = jnp.concatenate(corners + [jnp.zeros((3, LANES), f32)], 0)
+        edge[40:48] = extra[:8]
 
 
 def columns(whole, col_high, col_low):

time: 28 us -> 27.7 us (0.989)
  waiting for transfers between devices: 9.7 us -> 8.5 us
  starting transfers between devices: 11.4 us -> 12.3 us
    ppermute x6, starting transfers between devices: 9.3 us -> 10.2 us  [exchange(): received[k] = lax.ppermute(messages[k], axis, pairs)]
    ppermute x1, waiting for transfers between devices: 3.21 us -> 2.27 us  [per_device(): incoming = lax.ppermute(edge, 'gx', [(i, (i + 1) % 8) for i in range(8)])]
where the time goes in v2:
time: 27.7 us; the launch traced here: 27.6 us
  starting transfers between devices  12.3 us (44%)
  waiting for transfers between devices  8.5 us (31%)
  Pallas kernels  6.05 us (22%)
  between operations  0.7 us (3%)
    ppermute x6, starting transfers between devices, exchange(): received[k] = lax.ppermute(messages[k], axis, pairs)  10.2 us
    ppermute x6, waiting for transfers between devices, exchange(): received[k] = lax.ppermute(messages[k], axis, pairs)  6.23 us
    pallas_call x1, Pallas kernels, per_device(): pl.pallas_call(restrict_kernel, out_shape=jax.ShapeDtypeStruct((4, BLOCK,...  2.55 us
    pallas_call x1, Pallas kernels, per_device(): pl.pallas_call(edge_kernel, in_specs=[pl.BlockSpec(memory_space=pltpu.HBM...  2.45 us
    ppermute x1, waiting for transfers between devices, per_device(): incoming = lax.ppermute(edge, 'gx', [(i, (i + 1) % 8) for i in range(8)])  2.27 us
    ppermute x1, starting transfers between devices, per_device(): incoming = lax.ppermute(edge, 'gx', [(i, (i + 1) % 8) for i in range(8)])  2.09 us
    pallas_call x1, Pallas kernels, per_device(): pl.pallas_call(tension_kernel, out_shape=[result, result], scratch_shapes...  0.85 us
  transfers between devices with their start and end apart: 7, of which 5 were waited for; matrix products, arithmetic and copies ran while one was open for 0% of the time, Pallas kernels for 9%

profile of v2, /device:TPU:1, one launch (start us, length us, event | category | flops | bytes accessed | tf_op | source)
XLA Modules:
  0.0 27.6 jit_solution(8891713961115445639)
XLA Ops:
  0.6 0.0 copy-start.1
  0.6 0.0 copy-start
  0.7 2.5 %edge.1 = (f32[48,128]{1,0:T(8,128)S(1)}, f32[16,128]{1,0:T(8,128)S(1)}, f32[16,128]{1,0:T(8,128)S(1)}, bf16[512,256]{1,0:T(8,128)(2,1)S(1)}, bf16[512,256]{1,0:T(8,128)(2,1)S(1)}) custom-call(f32[8,32,32,128]{3,2,1,0:T(8,128)} %calcium.3, f32[8,32,32,128]{3,2,1,0:T(8,128)} %activation.3, s32[256]{0:T(256)} %element_first.1, f32[256]{0:T(256)} %offset_first.1, ...), custom_call_target="tpu_custom_call" | custom-call | tf_op jit(solution)/shard_map/edge/pallas_call | solution.py:410
  3.1 2.1 %collective-permute-start = (f32[48,128]{1,0:T(8,128)S(1)}, f32[48,128]{1,0:T(8,128)S(1)}, u32[]{:S(2)}, u32[]{:S(2)}) collective-permute-start(f32[48,128]{1,0:T(8,128)S(1)} %get-tuple-element.19), channel_id=1, source_target_pairs={{0,16},{16,32},{32,48},{48,64},{64,80},{80,96},{96,112},{112,0},{1... | collective-permute-start | bytes 73736 | tf_op jit(solution)/shard_map/ppermute | solution.py:432
  5.2 0.0 copy-start.4
  5.2 0.0 copy-start.5
  5.2 2.5 %restrict.1.blocks = f32[4,104,128]{2,1,0:T(8,128)S(1)} custom-call(f32[8,32,32,128]{3,2,1,0:T(8,128)S(1)} %copy-done, f32[8,32,32,128]{3,2,1,0:T(8,128)S(1)} %copy-done.1, f32[16,128]{1,0:T(8,128)S(1)} %get-tuple-element.15.first_weight, f32[16,128]{1,0:T(8,128)S(1)} %get-tuple-element.16.depth_weight, bf16[512,256]{1,0:T(8,128)(2,1)S(1)} %get-tuple-element.17.col_high, ...), custom_call_target="tpu_custom_call" | custom-call | tf_op jit(solution)/shard_map/restrict/pallas_call | solution.py:433
  7.8 2.3 %collective-permute-done.incoming = f32[48,128]{1,0:T(8,128)S(1)} collective-permute-done((f32[48,128]{1,0:T(8,128)S(1)}, f32[48,128]{1,0:T(8,128)S(1)}, u32[]{:S(2)}, u32[]{:S(2)}) %collective-permute-start) | collective-permute-done | bytes 24608 | tf_op jit(solution)/shard_map/ppermute | solution.py:432
  10.1 0.1 route.1
  10.2 3.2 %collective-permute-start.2 = (f32[104,128]{1,0:T(8,128)S(1)}, f32[104,128]{1,0:T(8,128)S(1)}, u32[]{:S(2)}, u32[]{:S(2)}) collective-permute-start(f32[104,128]{1,0:T(8,128)S(1)} %get-tuple-element.22), channel_id=1, source_target_pairs={{0,2},{1,3},{2,0},{3,1},{4,6},{5,7},{6,4},{7,5},{8,10},{9,11},{10,... | collective-permute-start | bytes 159752 | tf_op jit(solution)/shard_map/ppermute | solution.py:379
  13.4 0.8 %collective-permute-start.3 = (f32[104,128]{1,0:T(8,128)S(1)}, f32[104,128]{1,0:T(8,128)S(1)}, u32[]{:S(2)}, u32[]{:S(2)}) collective-permute-start(f32[104,128]{1,0:T(8,128)S(1)} %get-tuple-element.23), channel_id=1, source_target_pairs={{0,3},{1,0},{2,1},{3,2},{4,7},{5,4},{6,5},{7,6},{8,11},{9,8},{10,9... | collective-permute-start | bytes 159752 | tf_op jit(solution)/shard_map/ppermute | solution.py:379
  14.1 0.7 %collective-permute-start.1 = (f32[72,128]{1,0:T(8,128)S(1)}, f32[72,128]{1,0:T(8,128)S(1)}, u32[]{:S(2)}, u32[]{:S(2)}) collective-permute-start(f32[72,128]{1,0:T(8,128)S(1)} %get-tuple-element.21), channel_id=1, source_target_pairs={{0,1},{1,2},{2,3},{3,0},{4,5},{5,6},{6,7},{7,4},{8,9},{9,10},{10,1... | collective-permute-start | bytes 110600 | tf_op jit(solution)/shard_map/ppermute | solution.py:379
  14.8 3.3 %collective-permute-done.1.one = f32[72,128]{1,0:T(8,128)S(1)} collective-permute-done((f32[72,128]{1,0:T(8,128)S(1)}, f32[72,128]{1,0:T(8,128)S(1)}, u32[]{:S(2)}, u32[]{:S(2)}) %collective-permute-start.1) | collective-permute-done | bytes 36896 | tf_op jit(solution)/shard_map/ppermute | solution.py:379
  18.2 0.0 collective-permute-done.2.two
  18.2 0.0 collective-permute-done.3.three
  18.2 0.1 combine.1
  18.3 5.1 %collective-permute-start.4 = (f32[72,128]{1,0:T(8,128)S(1)}, f32[72,128]{1,0:T(8,128)S(1)}, u32[]{:S(2)}, u32[]{:S(2)}) collective-permute-start(f32[72,128]{1,0:T(8,128)S(1)} %get-tuple-element.25), channel_id=1, source_target_pairs={{0,4},{4,8},{8,12},{12,0},{1,5},{5,9},{9,13},{13,1},{2,6},{6,10},{... | collective-permute-start | bytes 110600 | tf_op jit(solution)/shard_map/ppermute | solution.py:379
  23.4 0.0 collective-permute-start.5
  23.4 0.5 %collective-permute-start.6 = (f32[72,128]{1,0:T(8,128)S(1)}, f32[72,128]{1,0:T(8,128)S(1)}, u32[]{:S(2)}, u32[]{:S(2)}) collective-permute-start(f32[72,128]{1,0:T(8,128)S(1)} %get-tuple-element.27), channel_id=1, source_target_pairs={{0,12},{4,0},{8,4},{12,8},{1,13},{5,1},{9,5},{13,9},{2,14},{6,2},{... | collective-permute-start | bytes 110600 | tf_op jit(solution)/shard_map/ppermute | solution.py:379
  23.8 0.6 %collective-permute-done.4.one = f32[72,128]{1,0:T(8,128)S(1)} collective-permute-done((f32[72,128]{1,0:T(8,128)S(1)}, f32[72,128]{1,0:T(8,128)S(1)}, u32[]{:S(2)}, u32[]{:S(2)}) %collective-permute-start.4) | collective-permute-done | bytes 36896 | tf_op jit(solution)/shard_map/ppermute | solution.py:379
  24.4 1.7 %collective-permute-done.5.two = f32[72,128]{1,0:T(8,128)S(1)} collective-permute-done((f32[72,128]{1,0:T(8,128)S(1)}, f32[72,128]{1,0:T(8,128)S(1)}, u32[]{:S(2)}, u32[]{:S(2)}) %collective-permute-start.5) | collective-permute-done | bytes 36896 | tf_op jit(solution)/shard_map/ppermute | solution.py:379
  26.2 0.6 %collective-permute-done.6.three = f32[72,128]{1,0:T(8,128)S(1)} collective-permute-done((f32[72,128]{1,0:T(8,128)S(1)}, f32[72,128]{1,0:T(8,128)S(1)}, u32[]{:S(2)}, u32[]{:S(2)}) %collective-permute-start.6) | collective-permute-done | bytes 36896 | tf_op jit(solution)/shard_map/ppermute | solution.py:379
  26.7 0.0 copy-done.2
  26.8 0.8 %tension.2 = (f32[8,2,128]{2,1,0:T(2,128)}, f32[8,2,128]{2,1,0:T(2,128)}) custom-call(f32[72,128]{1,0:T(8,128)S(1)} %get-tuple-element.24.own, f32[72,128]{1,0:T(8,128)S(1)} %collective-permute-done.4.one, f32[72,128]{1,0:T(8,128)S(1)} %collective-permute-done.5.two, f32[72,128]{1,0:T(8,128)S(1)} %collective-permute-done.6.three, ...), custom_call_target="tpu_custom_call" | custom-call | tf_op jit(solution)/shard_map/tension/pallas_call | solution.py:457
  (7 shorter events, 0.0 us)
Async XLA Ops:
  0.6 4.6 %copy-start.1 = (f32[8,32,32,128]{3,2,1,0:T(8,128)S(1)}, f32[8,32,32,128]{3,2,1,0:T(8,128)}, u32[]{:S(2)}) copy-start(f32[8,32,32,128]{3,2,1,0:T(8,128)} %activation.3) | copy-start | bytes 12582916
  0.6 4.6 %copy-start = (f32[8,32,32,128]{3,2,1,0:T(8,128)S(1)}, f32[8,32,32,128]{3,2,1,0:T(8,128)}, u32[]{:S(2)}) copy-start(f32[8,32,32,128]{3,2,1,0:T(8,128)} %calcium.3) | copy-start | bytes 12582916
  3.1 7.0 %collective-permute-start = (f32[48,128]{1,0:T(8,128)S(1)}, f32[48,128]{1,0:T(8,128)S(1)}, u32[]{:S(2)}, u32[]{:S(2)}) collective-permute-start(f32[48,128]{1,0:T(8,128)S(1)} %get-tuple-element.19), channel_id=1, source_target_pairs={{0,16},{16,32},{32,48},{48,64},{64,80},{80,96},{96,112},{112,0},{1... | collective-permute-start | bytes 73736 | tf_op jit(solution)/shard_map/ppermute | solution.py:432
  5.2 21.5 %copy-start.2 = (f32[8,2,128]{2,1,0:T(2,128)S(1)}, f32[8,2,128]{2,1,0:T(2,128)}, u32[]{:S(2)}) copy-start(f32[8,2,128]{2,1,0:T(2,128)} %troponin.1) | copy-start | bytes 24580
  5.2 21.5 %copy-start.3 = (f32[8,2,128]{2,1,0:T(2,128)S(1)}, f32[8,2,128]{2,1,0:T(2,128)}, u32[]{:S(2)}) copy-start(f32[8,2,128]{2,1,0:T(2,128)} %tension.3) | copy-start | bytes 24580
  5.2 21.5 %copy-start.4 = (f32[8,2,128]{2,1,0:T(2,128)S(1)}, f32[8,2,128]{2,1,0:T(2,128)}, u32[]{:S(2)}) copy-start(f32[8,2,128]{2,1,0:T(2,128)} %unbind.1) | copy-start | bytes 24580
  5.2 21.5 %copy-start.5 = (f32[8,2,128]{2,1,0:T(2,128)S(1)}, f32[8,2,128]{2,1,0:T(2,128)}, u32[]{:S(2)}) copy-start(f32[8,2,128]{2,1,0:T(2,128)} %relax.1) | copy-start | bytes 24580
  10.2 8.0 %collective-permute-start.2 = (f32[104,128]{1,0:T(8,128)S(1)}, f32[104,128]{1,0:T(8,128)S(1)}, u32[]{:S(2)}, u32[]{:S(2)}) collective-permute-start(f32[104,128]{1,0:T(8,128)S(1)} %get-tuple-element.22), channel_id=1, source_target_pairs={{0,2},{1,3},{2,0},{3,1},{4,6},{5,7},{6,4},{7,5},{8,10},{9,11},{10,... | collective-permute-start | bytes 159752 | tf_op jit(solution)/shard_map/ppermute | solution.py:379
  13.4 4.8 %collective-permute-start.3 = (f32[104,128]{1,0:T(8,128)S(1)}, f32[104,128]{1,0:T(8,128)S(1)}, u32[]{:S(2)}, u32[]{:S(2)}) collective-permute-start(f32[104,128]{1,0:T(8,128)S(1)} %get-tuple-element.23), channel_id=1, source_target_pairs={{0,3},{1,0},{2,1},{3,2},{4,7},{5,4},{6,5},{7,6},{8,11},{9,8},{10,9... | collective-permute-start | bytes 159752 | tf_op jit(solution)/shard_map/ppermute | solution.py:379
  14.1 4.0 %collective-permute-start.1 = (f32[72,128]{1,0:T(8,128)S(1)}, f32[72,128]{1,0:T(8,128)S(1)}, u32[]{:S(2)}, u32[]{:S(2)}) collective-permute-start(f32[72,128]{1,0:T(8,128)S(1)} %get-tuple-element.21), channel_id=1, source_target_pairs={{0,1},{1,2},{2,3},{3,0},{4,5},{5,6},{6,7},{7,4},{8,9},{9,10},{10,1... | collective-permute-start | bytes 110600 | tf_op jit(solution)/shard_map/ppermute | solution.py:379
  18.3 6.1 %collective-permute-start.4 = (f32[72,128]{1,0:T(8,128)S(1)}, f32[72,128]{1,0:T(8,128)S(1)}, u32[]{:S(2)}, u32[]{:S(2)}) collective-permute-start(f32[72,128]{1,0:T(8,128)S(1)} %get-tuple-element.25), channel_id=1, source_target_pairs={{0,4},{4,8},{8,12},{12,0},{1,5},{5,9},{9,13},{13,1},{2,6},{6,10},{... | collective-permute-start | bytes 110600 | tf_op jit(solution)/shard_map/ppermute | solution.py:379
  23.4 2.8 %collective-permute-start.5 = (f32[72,128]{1,0:T(8,128)S(1)}, f32[72,128]{1,0:T(8,128)S(1)}, u32[]{:S(2)}, u32[]{:S(2)}) collective-permute-start(f32[72,128]{1,0:T(8,128)S(1)} %get-tuple-element.26), channel_id=1, source_target_pairs={{0,8},{4,12},{8,0},{12,4},{1,9},{5,13},{9,1},{13,5},{2,10},{6,14},... | collective-permute-start | bytes 110600 | tf_op jit(solution)/shard_map/ppermute | solution.py:379
  23.4 3.4 %collective-permute-start.6 = (f32[72,128]{1,0:T(8,128)S(1)}, f32[72,128]{1,0:T(8,128)S(1)}, u32[]{:S(2)}, u32[]{:S(2)}) collective-permute-start(f32[72,128]{1,0:T(8,128)S(1)} %get-tuple-element.27), channel_id=1, source_target_pairs={{0,12},{4,0},{8,4},{12,8},{1,13},{5,1},{9,5},{13,9},{2,14},{6,2},{... | collective-permute-start | bytes 110600 | tf_op jit(solution)/shard_map/ppermute | solution.py:379

commit v3 on v2

--- a/solution.py
+++ b/solution.py
@@ -20,6 +20,7 @@
 ROWS = 72
 BLOCK = 104
 SURE = 26
+PAIRS = (SURE + 1 - (NODES - 1)) // 2
 PIECE = 72
 
 
@@ -420,11 +421,11 @@
         scratch_shapes=[line(x.shape[0], x.dtype) for x in vectors]
         + [
             pltpu.VMEM((2, SUBS, 32 - SURE, 32, LANES), f32),
-            pltpu.VMEM((SURE // 2, 2, SUBS, 2, 32, LANES), f32),
+            pltpu.VMEM((PAIRS, 2, SUBS, 2, 32, LANES), f32),
             pltpu.VMEM((32, 2048), f32),
             pltpu.SemaphoreType.DMA((6,)),
             pltpu.SemaphoreType.DMA,
-            pltpu.SemaphoreType.DMA((SURE // 2,)),
+            pltpu.SemaphoreType.DMA((PAIRS,)),
         ],
         compiler_params=pltpu.CompilerParams(vmem_limit_bytes=16 << 20),
         name="edge",

time: 27.7 us -> 27.7 us (level)
  no operation moved by 1% of the time
where the time goes in v3:
time: 27.7 us; the launch traced here: 27.6 us
  starting transfers between devices  12.3 us (44%)
  waiting for transfers between devices  8.5 us (31%)
  Pallas kernels  6.02 us (22%)
  between operations  0.7 us (3%)
    ppermute x6, starting transfers between devices, exchange(): received[k] = lax.ppermute(messages[k], axis, pairs)  10.2 us
    ppermute x6, waiting for transfers between devices, exchange(): received[k] = lax.ppermute(messages[k], axis, pairs)  6.23 us
    pallas_call x1, Pallas kernels, per_device(): pl.pallas_call(restrict_kernel, out_shape=jax.ShapeDtypeStruct((4, BLOCK,...  2.54 us
    pallas_call x1, Pallas kernels, per_device(): pl.pallas_call(edge_kernel, in_specs=[pl.BlockSpec(memory_space=pltpu.HBM...  2.43 us
    ppermute x1, waiting for transfers between devices, per_device(): incoming = lax.ppermute(edge, 'gx', [(i, (i + 1) % 8) for i in range(8)])  2.27 us
    ppermute x1, starting transfers between devices, per_device(): incoming = lax.ppermute(edge, 'gx', [(i, (i + 1) % 8) for i in range(8)])  2.09 us
    pallas_call x1, Pallas kernels, per_device(): pl.pallas_call(tension_kernel, out_shape=[result, result], scratch_shapes...  0.85 us
  transfers between devices with their start and end apart: 7, of which 5 were waited for; matrix products, arithmetic and copies ran while one was open for 0% of the time, Pallas kernels for 9%

profile of v3, /device:TPU:1, one launch (start us, length us, event | category | flops | bytes accessed | tf_op | source)
XLA Modules:
  0.0 27.6 jit_solution(11673896298834344156)
XLA Ops:
  0.6 0.0 copy-start.1
  0.7 2.4 %edge.1 = (f32[48,128]{1,0:T(8,128)S(1)}, f32[16,128]{1,0:T(8,128)S(1)}, f32[16,128]{1,0:T(8,128)S(1)}, bf16[512,256]{1,0:T(8,128)(2,1)S(1)}, bf16[512,256]{1,0:T(8,128)(2,1)S(1)}) custom-call(f32[8,32,32,128]{3,2,1,0:T(8,128)} %calcium.3, f32[8,32,32,128]{3,2,1,0:T(8,128)} %activation.3, s32[256]{0:T(256)} %element_first.1, f32[256]{0:T(256)} %offset_first.1, ...), custom_call_target="tpu_custom_call" | custom-call | tf_op jit(solution)/shard_map/edge/pallas_call | solution.py:411
  3.1 2.1 %collective-permute-start = (f32[48,128]{1,0:T(8,128)S(1)}, f32[48,128]{1,0:T(8,128)S(1)}, u32[]{:S(2)}, u32[]{:S(2)}) collective-permute-start(f32[48,128]{1,0:T(8,128)S(1)} %get-tuple-element.19), channel_id=1, source_target_pairs={{0,16},{16,32},{32,48},{48,64},{64,80},{80,96},{96,112},{112,0},{1... | collective-permute-start | bytes 73736 | tf_op jit(solution)/shard_map/ppermute | solution.py:433
  5.2 0.0 copy-start.4
  5.2 0.0 copy-start.5
  5.2 2.5 %restrict.1.blocks = f32[4,104,128]{2,1,0:T(8,128)S(1)} custom-call(f32[8,32,32,128]{3,2,1,0:T(8,128)S(1)} %copy-done, f32[8,32,32,128]{3,2,1,0:T(8,128)S(1)} %copy-done.1, f32[16,128]{1,0:T(8,128)S(1)} %get-tuple-element.15.first_weight, f32[16,128]{1,0:T(8,128)S(1)} %get-tuple-element.16.depth_weight, bf16[512,256]{1,0:T(8,128)(2,1)S(1)} %get-tuple-element.17.col_high, ...), custom_call_target="tpu_custom_call" | custom-call | tf_op jit(solution)/shard_map/restrict/pallas_call | solution.py:434
  7.8 2.3 %collective-permute-done.incoming = f32[48,128]{1,0:T(8,128)S(1)} collective-permute-done((f32[48,128]{1,0:T(8,128)S(1)}, f32[48,128]{1,0:T(8,128)S(1)}, u32[]{:S(2)}, u32[]{:S(2)}) %collective-permute-start) | collective-permute-done | bytes 24608 | tf_op jit(solution)/shard_map/ppermute | solution.py:433
  10.0 0.1 route.1
  10.1 3.2 %collective-permute-start.2 = (f32[104,128]{1,0:T(8,128)S(1)}, f32[104,128]{1,0:T(8,128)S(1)}, u32[]{:S(2)}, u32[]{:S(2)}) collective-permute-start(f32[104,128]{1,0:T(8,128)S(1)} %get-tuple-element.22), channel_id=1, source_target_pairs={{0,2},{1,3},{2,0},{3,1},{4,6},{5,7},{6,4},{7,5},{8,10},{9,11},{10,... | collective-permute-start | bytes 159752 | tf_op jit(solution)/shard_map/ppermute | solution.py:380
  13.3 0.8 %collective-permute-start.3 = (f32[104,128]{1,0:T(8,128)S(1)}, f32[104,128]{1,0:T(8,128)S(1)}, u32[]{:S(2)}, u32[]{:S(2)}) collective-permute-start(f32[104,128]{1,0:T(8,128)S(1)} %get-tuple-element.23), channel_id=1, source_target_pairs={{0,3},{1,0},{2,1},{3,2},{4,7},{5,4},{6,5},{7,6},{8,11},{9,8},{10,9... | collective-permute-start | bytes 159752 | tf_op jit(solution)/shard_map/ppermute | solution.py:380
  14.1 0.7 %collective-permute-start.1 = (f32[72,128]{1,0:T(8,128)S(1)}, f32[72,128]{1,0:T(8,128)S(1)}, u32[]{:S(2)}, u32[]{:S(2)}) collective-permute-start(f32[72,128]{1,0:T(8,128)S(1)} %get-tuple-element.21), channel_id=1, source_target_pairs={{0,1},{1,2},{2,3},{3,0},{4,5},{5,6},{6,7},{7,4},{8,9},{9,10},{10,1... | collective-permute-start | bytes 110600 | tf_op jit(solution)/shard_map/ppermute | solution.py:380
  14.8 3.3 %collective-permute-done.1.one = f32[72,128]{1,0:T(8,128)S(1)} collective-permute-done((f32[72,128]{1,0:T(8,128)S(1)}, f32[72,128]{1,0:T(8,128)S(1)}, u32[]{:S(2)}, u32[]{:S(2)}) %collective-permute-start.1) | collective-permute-done | bytes 36896 | tf_op jit(solution)/shard_map/ppermute | solution.py:380
  18.1 0.0 collective-permute-done.2.two
  18.1 0.0 collective-permute-done.3.three
  18.1 0.1 combine.1
  18.3 5.1 %collective-permute-start.4 = (f32[72,128]{1,0:T(8,128)S(1)}, f32[72,128]{1,0:T(8,128)S(1)}, u32[]{:S(2)}, u32[]{:S(2)}) collective-permute-start(f32[72,128]{1,0:T(8,128)S(1)} %get-tuple-element.25), channel_id=1, source_target_pairs={{0,4},{4,8},{8,12},{12,0},{1,5},{5,9},{9,13},{13,1},{2,6},{6,10},{... | collective-permute-start | bytes 110600 | tf_op jit(solution)/shard_map/ppermute | solution.py:380
  23.3 0.0 collective-permute-start.5
  23.3 0.5 %collective-permute-start.6 = (f32[72,128]{1,0:T(8,128)S(1)}, f32[72,128]{1,0:T(8,128)S(1)}, u32[]{:S(2)}, u32[]{:S(2)}) collective-permute-start(f32[72,128]{1,0:T(8,128)S(1)} %get-tuple-element.27), channel_id=1, source_target_pairs={{0,12},{4,0},{8,4},{12,8},{1,13},{5,1},{9,5},{13,9},{2,14},{6,2},{... | collective-permute-start | bytes 110600 | tf_op jit(solution)/shard_map/ppermute | solution.py:380
  23.8 0.6 %collective-permute-done.4.one = f32[72,128]{1,0:T(8,128)S(1)} collective-permute-done((f32[72,128]{1,0:T(8,128)S(1)}, f32[72,128]{1,0:T(8,128)S(1)}, u32[]{:S(2)}, u32[]{:S(2)}) %collective-permute-start.4) | collective-permute-done | bytes 36896 | tf_op jit(solution)/shard_map/ppermute | solution.py:380
  24.4 1.7 %collective-permute-done.5.two = f32[72,128]{1,0:T(8,128)S(1)} collective-permute-done((f32[72,128]{1,0:T(8,128)S(1)}, f32[72,128]{1,0:T(8,128)S(1)}, u32[]{:S(2)}, u32[]{:S(2)}) %collective-permute-start.5) | collective-permute-done | bytes 36896 | tf_op jit(solution)/shard_map/ppermute | solution.py:380
  26.1 0.6 %collective-permute-done.6.three = f32[72,128]{1,0:T(8,128)S(1)} collective-permute-done((f32[72,128]{1,0:T(8,128)S(1)}, f32[72,128]{1,0:T(8,128)S(1)}, u32[]{:S(2)}, u32[]{:S(2)}) %collective-permute-start.6) | collective-permute-done | bytes 36896 | tf_op jit(solution)/shard_map/ppermute | solution.py:380
  26.7 0.0 copy-done.2
  26.7 0.0 copy-done.4
  26.7 0.8 %tension.2 = (f32[8,2,128]{2,1,0:T(2,128)}, f32[8,2,128]{2,1,0:T(2,128)}) custom-call(f32[72,128]{1,0:T(8,128)S(1)} %get-tuple-element.24.own, f32[72,128]{1,0:T(8,128)S(1)} %collective-permute-done.4.one, f32[72,128]{1,0:T(8,128)S(1)} %collective-permute-done.5.two, f32[72,128]{1,0:T(8,128)S(1)} %collective-permute-done.6.three, ...), custom_call_target="tpu_custom_call" | custom-call | tf_op jit(solution)/shard_map/tension/pallas_call | solution.py:458
  (7 shorter events, 0.0 us)
Async XLA Ops:
  0.6 4.6 %copy-start.1 = (f32[8,32,32,128]{3,2,1,0:T(8,128)S(1)}, f32[8,32,32,128]{3,2,1,0:T(8,128)}, u32[]{:S(2)}) copy-start(f32[8,32,32,128]{3,2,1,0:T(8,128)} %activation.3) | copy-start | bytes 12582916
  0.6 4.5 %copy-start = (f32[8,32,32,128]{3,2,1,0:T(8,128)S(1)}, f32[8,32,32,128]{3,2,1,0:T(8,128)}, u32[]{:S(2)}) copy-start(f32[8,32,32,128]{3,2,1,0:T(8,128)} %calcium.3) | copy-start | bytes 12582916
  3.1 7.0 %collective-permute-start = (f32[48,128]{1,0:T(8,128)S(1)}, f32[48,128]{1,0:T(8,128)S(1)}, u32[]{:S(2)}, u32[]{:S(2)}) collective-permute-start(f32[48,128]{1,0:T(8,128)S(1)} %get-tuple-element.19), channel_id=1, source_target_pairs={{0,16},{16,32},{32,48},{48,64},{64,80},{80,96},{96,112},{112,0},{1... | collective-permute-start | bytes 73736 | tf_op jit(solution)/shard_map/ppermute | solution.py:433
  5.2 21.5 %copy-start.2 = (f32[8,2,128]{2,1,0:T(2,128)S(1)}, f32[8,2,128]{2,1,0:T(2,128)}, u32[]{:S(2)}) copy-start(f32[8,2,128]{2,1,0:T(2,128)} %troponin.1) | copy-start | bytes 24580
  5.2 21.5 %copy-start.3 = (f32[8,2,128]{2,1,0:T(2,128)S(1)}, f32[8,2,128]{2,1,0:T(2,128)}, u32[]{:S(2)}) copy-start(f32[8,2,128]{2,1,0:T(2,128)} %tension.3) | copy-start | bytes 24580
  5.2 21.5 %copy-start.4 = (f32[8,2,128]{2,1,0:T(2,128)S(1)}, f32[8,2,128]{2,1,0:T(2,128)}, u32[]{:S(2)}) copy-start(f32[8,2,128]{2,1,0:T(2,128)} %unbind.1) | copy-start | bytes 24580
  5.2 21.5 %copy-start.5 = (f32[8,2,128]{2,1,0:T(2,128)S(1)}, f32[8,2,128]{2,1,0:T(2,128)}, u32[]{:S(2)}) copy-start(f32[8,2,128]{2,1,0:T(2,128)} %relax.1) | copy-start | bytes 24580
  10.1 8.0 %collective-permute-start.2 = (f32[104,128]{1,0:T(8,128)S(1)}, f32[104,128]{1,0:T(8,128)S(1)}, u32[]{:S(2)}, u32[]{:S(2)}) collective-permute-start(f32[104,128]{1,0:T(8,128)S(1)} %get-tuple-element.22), channel_id=1, source_target_pairs={{0,2},{1,3},{2,0},{3,1},{4,6},{5,7},{6,4},{7,5},{8,10},{9,11},{10,... | collective-permute-start | bytes 159752 | tf_op jit(solution)/shard_map/ppermute | solution.py:380
  13.3 4.8 %collective-permute-start.3 = (f32[104,128]{1,0:T(8,128)S(1)}, f32[104,128]{1,0:T(8,128)S(1)}, u32[]{:S(2)}, u32[]{:S(2)}) collective-permute-start(f32[104,128]{1,0:T(8,128)S(1)} %get-tuple-element.23), channel_id=1, source_target_pairs={{0,3},{1,0},{2,1},{3,2},{4,7},{5,4},{6,5},{7,6},{8,11},{9,8},{10,9... | collective-permute-start | bytes 159752 | tf_op jit(solution)/shard_map/ppermute | solution.py:380
  14.1 4.0 %collective-permute-start.1 = (f32[72,128]{1,0:T(8,128)S(1)}, f32[72,128]{1,0:T(8,128)S(1)}, u32[]{:S(2)}, u32[]{:S(2)}) collective-permute-start(f32[72,128]{1,0:T(8,128)S(1)} %get-tuple-element.21), channel_id=1, source_target_pairs={{0,1},{1,2},{2,3},{3,0},{4,5},{5,6},{6,7},{7,4},{8,9},{9,10},{10,1... | collective-permute-start | bytes 110600 | tf_op jit(solution)/shard_map/ppermute | solution.py:380
  18.3 6.1 %collective-permute-start.4 = (f32[72,128]{1,0:T(8,128)S(1)}, f32[72,128]{1,0:T(8,128)S(1)}, u32[]{:S(2)}, u32[]{:S(2)}) collective-permute-start(f32[72,128]{1,0:T(8,128)S(1)} %get-tuple-element.25), channel_id=1, source_target_pairs={{0,4},{4,8},{8,12},{12,0},{1,5},{5,9},{9,13},{13,1},{2,6},{6,10},{... | collective-permute-start | bytes 110600 | tf_op jit(solution)/shard_map/ppermute | solution.py:380
  23.3 2.8 %collective-permute-start.5 = (f32[72,128]{1,0:T(8,128)S(1)}, f32[72,128]{1,0:T(8,128)S(1)}, u32[]{:S(2)}, u32[]{:S(2)}) collective-permute-start(f32[72,128]{1,0:T(8,128)S(1)} %get-tuple-element.26), channel_id=1, source_target_pairs={{0,8},{4,12},{8,0},{12,4},{1,9},{5,13},{9,1},{13,5},{2,10},{6,14},... | collective-permute-start | bytes 110600 | tf_op jit(solution)/shard_map/ppermute | solution.py:380
  23.3 3.4 %collective-permute-start.6 = (f32[72,128]{1,0:T(8,128)S(1)}, f32[72,128]{1,0:T(8,128)S(1)}, u32[]{:S(2)}, u32[]{:S(2)}) collective-permute-start(f32[72,128]{1,0:T(8,128)S(1)} %get-tuple-element.27), channel_id=1, source_target_pairs={{0,12},{4,0},{8,4},{12,8},{1,13},{5,1},{9,5},{13,9},{2,14},{6,2},{... | collective-permute-start | bytes 110600 | tf_op jit(solution)/shard_map/ppermute | solution.py:380
